TPU v7x, 128 devices: a whole 4x4x4 slice. The times are simulated.
128 devices in a mesh: lat: 8 (over z, core), lon: 16 (over y, x).
Axes of the slice: x: 4, y: 4, z: 4, core: 2. Of those that a mesh axis runs over, the one named last changes fastest.
Arguments:
- increments: bfloat16 [262144, 3, 128], P(('lat', 'lon')), may hold values from -6 to 6
- cotangent: bfloat16 [262144, 128], P(('lat', 'lon')), may hold values from -6 to 6
- owner_perm: int32 [128, 2048], P(('lat', 'lon')), may hold values from 0 to 2047, each once within a row
- coarse_index: int32 [2, 131072], P(None, ('lat', 'lon')), may hold values from 0 to 2047
- coarse_weight: float32 [131072], P(('lat', 'lon')), may hold values from 0.2 to 0.8
- back_index: int32 [2, 262144], P(None, ('lat', 'lon')), may hold values from 0 to 1023
- back_weight: float32 [262144], P(('lat', 'lon')), may hold values from 0.2 to 0.8
- lw_scale: float32 [16, 131072], P(None, ('lat', 'lon')), may hold values from 0.1 to 1
- sw_scale: float32 [14, 131072], P(None, ('lat', 'lon')), may hold values from 0.2 to 2
- sunlit: int32 [131072], P(('lat', 'lon')), may hold values from 0 to 1, as said below
- lw_table: bfloat16 [16, 3, 128, 128], P(None, None, 'lon'), may hold values from -0.3125 to 0.3125
- sw_table: bfloat16 [14, 3, 128, 128], P(None, None, 'lon'), may hold values from -0.3125 to 0.3125
Outputs:
- tendency: bfloat16 [262144, 128], P(('lat', 'lon'))
- gradient: bfloat16 [262144, 3, 128], P(('lat', 'lon'))
Inputs may be any that keep to these rules, and one draw needn't show every extreme that they name: In each device's block of 1024 radiation columns at most 640 are sunlit, and some device has exactly 640.
All inputs are finite; a program needn't handle non-finite values.
Results may differ from a plain program's by a relative error of at most 0.014.
Values may be sent and summed in bfloat16 or wider, within the bound.
No kernel may reach another device: no remote copies, remote signals or barrier semaphores. Data moves between devices by JAX's collectives and lax.ppermute only.
A program may use at most 64 MiB of HBM per device.

v0:
```python
import jax
import jax.numpy as jnp
from jax import lax
from jax.sharding import PartitionSpec as P


def block_split(row_count):
    block = 512
    return (block, row_count // block)


def band_sum(coarse, band_table, band_scale):
    row_count = coarse.shape[0]
    block, blocks = block_split(row_count)
    coarse_blocks = coarse.reshape(blocks, block, coarse.shape[1])
    scale_blocks = band_scale.reshape(band_scale.shape[0], blocks, block).swapaxes(0, 1)

    def one_block(pair):
        product = jnp.einsum("rc,bck->rbk", pair[0], band_table, preferred_element_type=jnp.float32)
        return jnp.einsum("br,rbk->rk", pair[1], product)

    return lax.map(one_block, (coarse_blocks, scale_blocks)).reshape(row_count, band_table.shape[2])


def band_adjoint(adjoint_coarse, band_table, band_scale):
    row_count = adjoint_coarse.shape[0]
    block, blocks = block_split(row_count)
    adjoint_blocks = adjoint_coarse.reshape(blocks, block, adjoint_coarse.shape[1])
    scale_blocks = band_scale.reshape(band_scale.shape[0], blocks, block).swapaxes(0, 1)

    def one_block(pair):
        lifted = (pair[1].T[:, :, None] * pair[0][:, None, :]).astype(jnp.bfloat16)
        return jnp.einsum("rbk,bck->rc", lifted, band_table, preferred_element_type=jnp.float32)

    return lax.map(one_block, (adjoint_blocks, scale_blocks)).reshape(
        row_count, band_table.shape[1]
    )


def spread_back(values, index_pair, weight, target_count):
    source_count = values.shape[0]
    block, blocks = block_split(source_count)
    width = values.shape[1]
    targets = jnp.arange(target_count, dtype=jnp.int32)

    def one_block(total, item):
        rows, first, second, share = item
        table = share[:, None] * (first[:, None] == targets[None, :]).astype(jnp.float32)
        table = table + (1.0 - share)[:, None] * (second[:, None] == targets[None, :]).astype(
            jnp.float32
        )
        added = jnp.einsum("nt,nw->tw", table, rows, preferred_element_type=jnp.float32)
        return (total + added, None)

    start = jnp.zeros((target_count, width), jnp.float32)
    items = (
        values.reshape(blocks, block, width),
        index_pair[0].reshape(blocks, block),
        index_pair[1].reshape(blocks, block),
        weight.reshape(blocks, block),
    )
    total, unused = lax.scan(one_block, start, items)
    return total


def local(
    increments,
    cotangent,
    owner_perm,
    coarse_index,
    coarse_weight,
    back_index,
    back_weight,
    lw_scale,
    sw_scale,
    sunlit,
    lw_table,
    sw_table,
):
    lw_full, sw_full = (
        lax.all_gather(lw_table, "lon", axis=2, tiled=True),
        lax.all_gather(sw_table, "lon", axis=2, tiled=True),
    )
    level_count = lw_full.shape[3]
    lw_bands = lw_full.reshape(lw_full.shape[0], -1, level_count)
    sw_bands = sw_full.reshape(sw_full.shape[0], -1, level_count)
    order_map = owner_perm[0]
    col_count = increments.shape[0]
    sent_fields = increments[order_map]
    sent_cotangent = cotangent[order_map]
    fields, cot_rad = (
        lax.all_to_all(sent_fields, ("lat", "lon"), split_axis=0, concat_axis=0, tiled=True),
        lax.all_to_all(sent_cotangent, ("lat", "lon"), split_axis=0, concat_axis=0, tiled=True),
    )
    row_count = coarse_weight.shape[0]
    flat_rows = fields.reshape(col_count, -1)
    first = flat_rows[coarse_index[0]].astype(jnp.float32)
    second = flat_rows[coarse_index[1]].astype(jnp.float32)
    coarse = (coarse_weight[:, None] * first + (1.0 - coarse_weight)[:, None] * second).astype(
        jnp.bfloat16
    )
    heating = band_sum(coarse, lw_bands, lw_scale)
    cot_float = cot_rad.astype(jnp.float32)
    adjoint_coarse = spread_back(cot_float, back_index, back_weight, row_count)
    adjoint_rows = band_adjoint(adjoint_coarse, lw_bands, lw_scale)
    sw_weight = sw_scale * sunlit.astype(jnp.float32)[None, :]
    heating = heating + band_sum(coarse, sw_bands, sw_weight)
    adjoint_rows = adjoint_rows + band_adjoint(adjoint_coarse, sw_bands, sw_weight)
    tendency_rad = (
        back_weight[:, None] * heating[back_index[0]]
        + (1.0 - back_weight)[:, None] * heating[back_index[1]]
    ).astype(jnp.bfloat16)
    gradient_rad = spread_back(adjoint_rows, coarse_index, coarse_weight, col_count).astype(
        jnp.bfloat16
    )
    gradient_rad = gradient_rad.reshape(increments.shape)
    back_tendency, back_gradient = (
        lax.all_to_all(tendency_rad, ("lat", "lon"), split_axis=0, concat_axis=0, tiled=True),
        lax.all_to_all(gradient_rad, ("lat", "lon"), split_axis=0, concat_axis=0, tiled=True),
    )
    inverse_map = (
        jnp.zeros((col_count,), jnp.int32).at[order_map].set(jnp.arange(col_count, dtype=jnp.int32))
    )
    tendency = back_tendency[inverse_map]
    gradient = back_gradient[inverse_map]
    return (tendency, gradient)


def solution(mesh):
    in_specs = (
        P(("lat", "lon"), None, None),
        P(("lat", "lon"), None),
        P(("lat", "lon"), None),
        P(None, ("lat", "lon")),
        P(("lat", "lon")),
        P(None, ("lat", "lon")),
        P(("lat", "lon")),
        P(None, ("lat", "lon")),
        P(None, ("lat", "lon")),
        P(("lat", "lon")),
        P(None, None, "lon", None),
        P(None, None, "lon", None),
    )
    out_specs = (P(("lat", "lon"), None), P(("lat", "lon"), None, None))
    return jax.shard_map(local, mesh=mesh, in_specs=in_specs, out_specs=out_specs, check_vma=False)
```

profile of v0, /device:TPU:1, one launch (start us, length us, event | category | flops | bytes accessed | tf_op | source)
XLA Modules:
  0.0 268.4 jit_solution(4165597984832605082)
XLA Ops:
  8.7 8.8 %gather_fusion.6 = bf16[2048,128]{1,0:T(8,128)(2,1)} fusion(bf16[2048,128]{1,0:T(8,128)(2,1)} %param.25, s32[2048]{0:T(1024)S(1)} %broadcast_clamp_fusion.2), kind=kCustom, calls=%fused_computation.6 | custom fusion | bytes 1056768 | tf_op jit(solution)/shard_map/gather | solution.py:90
  17.5 11.5 %all-to-all-start.2 = ((bf16[128,16,128]{2,1,0:T(8,128)(2,1)}), bf16[128,16,128]{2,1,0:T(8,128)(2,1)S(1)}, u32[]{:S(2)}, u32[]{:S(2)}) async-start(bf16[128,16,128]{2,1,0:T(8,128)(2,1)} %bitcast.45), calls=%async_computation.2 | async-start | bytes 1048576 | tf_op jit(solution)/shard_map/all_to_all | solution.py:93
  30.0 18.4 %gather_fusion = bf16[2048,3,128]{2,0,1:T(8,128)(2,1)} fusion(bf16[2048,3,128]{2,0,1:T(8,128)(2,1)S(1)} %copy-done, s32[2048]{0:T(1024)S(1)} %broadcast_clamp_fusion.2), kind=kCustom, calls=%fused_computation | custom fusion | bytes 3153920 | tf_op jit(solution)/shard_map/gather | solution.py:89
  48.4 4.2 %copy.25 = bf16[2048,3,128]{2,1,0:T(4,128)(2,1)} copy(bf16[2048,3,128]{2,0,1:T(8,128)(2,1)} %gather_fusion) | data formatting | bytes 3145728 | tf_op jit(solution)/shard_map/gather | solution.py:89
  53.1 10.2 %all-to-all-start = ((bf16[2048,3,128]{2,1,0:T(4,128)(2,1)}), bf16[2048,3,128]{2,1,0:T(4,128)(2,1)}, u32[]{:S(2)}, u32[]{:S(2)}) async-start(bf16[2048,3,128]{2,1,0:T(4,128)(2,1)} %copy.25), calls=%async_computation | async-start | bytes 4194304 | tf_op jit(solution)/shard_map/all_to_all | solution.py:92
  63.4 4.5 %while.68 = (s32[]{:T(128)}, f32[1024,128]{1,0:T(8,128)S(1)}, s32[4,512]{1,0:T(4,128)S(1)}, f32[4,512]{1,0:T(4,128)S(1)}, s32[4,512]{1,0:T(4,128)S(1)}, /*index=...) while((s32[]{:T(128)}, f32[1024,128]{1,0:T(8,128)S(1)}, s32[4,512]{1,0:T(4,128)S(1)}, ...), condition=%wide.region_6.7_spmd.clone.clone, body=%wide.region_5.6_spmd.clone.clone.sunk | while | flops 137101824 | bytes 1204331 | solution.py:62
  66.8 1.1 fusion.109
  67.9 26.3 %all-to-all-done = bf16[2048,3,128]{2,1,0:T(4,128)(2,1)} async-done(((bf16[2048,3,128]{2,1,0:T(4,128)(2,1)}), bf16[2048,3,128]{2,1,0:T(4,128)(2,1)}, u32[]{:S(2)}, u32[]{:S(2)}) %all-to-all-start) | async-done | bytes 1572896 | tf_op jit(solution)/shard_map/all_to_all | solution.py:92
  94.3 4.1 %copy.26 = bf16[2048,3,128]{0,2,1:T(8,128)(2,1)} copy(bf16[2048,3,128]{2,1,0:T(4,128)(2,1)} %all-to-all-done) | data formatting | bytes 3145728 | tf_op jit(solution)/shard_map/all_to_all | solution.py:92
  98.3 1.9 copy.27
  100.2 5.0 %gather_fusion.1 = bf16[1024,384]{1,0:T(8,128)(2,1)} fusion(bf16[2048,384]{1,0:T(8,128)(2,1)S(1)} %copy.27, s32[1024]{0:T(1024)S(1)} %broadcast_clamp_fusion.4), kind=kCustom, calls=%fused_computation.1 | custom fusion | bytes 1576960 | tf_op jit(solution)/shard_map/gather | solution.py:97
  105.3 5.0 %gather_fusion.2 = bf16[1024,384]{1,0:T(8,128)(2,1)} fusion(bf16[2048,384]{1,0:T(8,128)(2,1)S(1)} %copy.27, s32[1024]{0:T(1024)S(1)} %broadcast_clamp_fusion.3), kind=kCustom, calls=%fused_computation.2 | custom fusion | bytes 1576960 | tf_op jit(solution)/shard_map/gather | solution.py:98
  110.2 2.8 %fusion.58 = bf16[2,512,384]{2,1,0:T(8,128)(2,1)} fusion(bf16[2,512,384]{2,1,0:T(8,128)(2,1)} %bitcast.162, bf16[2,512,384]{2,1,0:T(8,128)(2,1)} %bitcast.161, f32[2,512]{1,0:T(2,128)S(1)} %mul.123, f32[2,512]{1,0:T(2,128)S(1)} %mul.120), kind=kLoop, calls=%fused_computation.85 | loop fusion | flops 2359296 | bytes 2367488 | tf_op jit(solution)/shard_map/convert_element_type | solution.py:99
  113.1 1.2 broadcast.138.clone.1
  114.3 6.9 %while.67 = (s32[]{:T(128)}, f32[2,512,384]{2,1,0:T(8,128)}, f32[2,14,512]{2,1,0:T(8,128)S(1)}, f32[2,512,128]{2,1,0:T(8,128)S(1)}, bf16[14,384,128]{2,1,0:T(8,128)(2,1)}, /*index=5*/s32[]{:T(128)}) while((s32[]{:T(128)}, f32[2,512,384]{2,1,0:T(8,128)}, f32[2,14,512]{2,1,0:T(8,128)S(1)}, f32[2,512,128]{2,1,0:T(8,128)S(1)}, ...), condition=%wide.region_10.11_spmd, body=%wide.region_9.10_spmd.sunk | while | flops 706478080 | bytes 3035725 | solution.py:35
  114.4 3.4 %fusion.106 = f32[2,512,384]{2,1,0:T(8,128)} fusion(f32[2,512,384]{2,1,0:T(8,128)} %get-tuple-element.693, s32[]{:T(128)} %get-tuple-element.692, bf16[14,384,128]{2,1,0:T(8,128)(2,1)} %get-tuple-element.702, f32[512,128]{1,0:T(8,128)S(1)} %dynamic-slice_bitcast_fusion.16, f32[512,14]{0,1:T(8,128)S(1)} %dynamic-slice_bitcast_fusion.17), kind=kOutput, calls=%fused_computation.40.clone.1 | convolution fusion | flops 706478080 | bytes 2454016 | tf_op jit(solution)/shard_map/while/body/eval_jaxpr/rbk,bck->rc/dot_general | solution.py:33
  117.8 3.4 %fusion.106 = f32[2,512,384]{2,1,0:T(8,128)} fusion(f32[2,512,384]{2,1,0:T(8,128)} %get-tuple-element.693, s32[]{:T(128)} %get-tuple-element.692, bf16[14,384,128]{2,1,0:T(8,128)(2,1)} %get-tuple-element.702, f32[512,128]{1,0:T(8,128)S(1)} %dynamic-slice_bitcast_fusion.16, f32[512,14]{0,1:T(8,128)S(1)} %dynamic-slice_bitcast_fusion.17), kind=kOutput, calls=%fused_computation.40.clone.1 | convolution fusion | flops 706478080 | bytes 2454016 | tf_op jit(solution)/shard_map/while/body/eval_jaxpr/rbk,bck->rc/dot_general | solution.py:33
  121.2 13.8 %while.65 = (s32[]{:T(128)}, f32[2,512,128]{2,1,0:T(8,128)S(1)}, bf16[2,14,512]{2,1,0:T(8,128)(2,1)S(1)}, bf16[2,512,384]{2,1,0:T(8,128)(2,1)}, bf16[14,384,128]{2,1,0:T(8,128)(2,1)}, /*index=5*/s32[]{:T(128)}) while((s32[]{:T(128)}, f32[2,512,128]{2,1,0:T(8,128)S(1)}, bf16[2,14,512]{2,1,0:T(8,128)(2,1)S(1)}, bf16[2,512,384]{2,1,0:T(8,128)(2,1)}, ...), condition=%wide.region_3.4_spmd, body=%wide.region_2.3_spmd.sunk | while | flops 706478080 | bytes 6298189 | solution.py:22
  121.2 3.8 %fusion.101 = bf16[512,14,128]{2,0,1:T(8,128)(2,1)} fusion(bf16[14,384,128]{2,1,0:T(8,128)(2,1)} %get-tuple-element.642, bf16[2,512,384]{2,1,0:T(8,128)(2,1)} %get-tuple-element.641, s32[]{:T(128)} %get-tuple-element.632), kind=kOutput, calls=%fused_computation.21.clone.1 | convolution fusion | flops 704643072 | bytes 3604992 | tf_op jit(solution)/shard_map/while/body/eval_jaxpr/rc,bck->rbk/dot_general | solution.py:19
  125.3 2.8 %fusion.102 = f32[512,1,128]{2,1,0:T(1,128)S(1)} fusion(bf16[14,512,1]{0,2,1:T(2,128)(2,1)S(1)} %copy.55, bf16[512,14,128]{2,0,1:T(8,128)(2,1)} %fusion.101), kind=kOutput, calls=%fused_computation.19.clone.1 | convolution fusion | flops 1835008 | bytes 2111488 | tf_op jit(solution)/shard_map/while/body/eval_jaxpr/br,rbk->rk/dot_general | solution.py:20
  128.1 3.8 %fusion.101 = bf16[512,14,128]{2,0,1:T(8,128)(2,1)} fusion(bf16[14,384,128]{2,1,0:T(8,128)(2,1)} %get-tuple-element.642, bf16[2,512,384]{2,1,0:T(8,128)(2,1)} %get-tuple-element.641, s32[]{:T(128)} %get-tuple-element.632), kind=kOutput, calls=%fused_computation.21.clone.1 | convolution fusion | flops 704643072 | bytes 3604992 | tf_op jit(solution)/shard_map/while/body/eval_jaxpr/rc,bck->rbk/dot_general | solution.py:19
  132.2 2.8 %fusion.102 = f32[512,1,128]{2,1,0:T(1,128)S(1)} fusion(bf16[14,512,1]{0,2,1:T(2,128)(2,1)S(1)} %copy.55, bf16[512,14,128]{2,0,1:T(8,128)(2,1)} %fusion.101), kind=kOutput, calls=%fused_computation.19.clone.1 | convolution fusion | flops 1835008 | bytes 2111488 | tf_op jit(solution)/shard_map/while/body/eval_jaxpr/br,rbk->rk/dot_general | solution.py:20
  135.9 16.2 %while.64 = (s32[]{:T(128)}, f32[2,512,128]{2,1,0:T(8,128)}, bf16[2,16,512]{2,1,0:T(8,128)(2,1)S(1)}, bf16[2,512,384]{2,1,0:T(8,128)(2,1)}, bf16[16,384,128]{2,1,0:T(8,128)(2,1)}, /*index=5*/s32[]{:T(128)}) while((s32[]{:T(128)}, f32[2,512,128]{2,1,0:T(8,128)}, bf16[2,16,512]{2,1,0:T(8,128)(2,1)S(1)}, bf16[2,512,384]{2,1,0:T(8,128)(2,1)}, ...), condition=%wide.region_1.2_spmd, body=%wide.region_0.1_spmd.sunk | while | flops 807403520 | bytes 7029833 | solution.py:22
  135.9 4.2 %fusion.95 = bf16[512,16,128]{2,0,1:T(8,128)(2,1)} fusion(bf16[16,384,128]{2,1,0:T(8,128)(2,1)} %get-tuple-element.624, bf16[2,512,384]{2,1,0:T(8,128)(2,1)} %get-tuple-element.623, s32[]{:T(128)} %get-tuple-element.614), kind=kOutput, calls=%fused_computation.13.clone.1 | convolution fusion | flops 805306368 | bytes 4063744 | tf_op jit(solution)/shard_map/while/body/eval_jaxpr/rc,bck->rbk/dot_general | solution.py:19
  140.2 3.0 %fusion.96 = f32[512,1,128]{2,1,0:T(1,128)S(1)} fusion(bf16[16,512,1]{0,2,1:T(2,128)(2,1)S(1)} %copy.53, bf16[512,16,128]{2,0,1:T(8,128)(2,1)} %fusion.95), kind=kOutput, calls=%fused_computation.11.clone.1 | convolution fusion | flops 2097152 | bytes 2375680 | tf_op jit(solution)/shard_map/while/body/eval_jaxpr/br,rbk->rk/dot_general | solution.py:20
  144.0 4.2 %fusion.95 = bf16[512,16,128]{2,0,1:T(8,128)(2,1)} fusion(bf16[16,384,128]{2,1,0:T(8,128)(2,1)} %get-tuple-element.624, bf16[2,512,384]{2,1,0:T(8,128)(2,1)} %get-tuple-element.623, s32[]{:T(128)} %get-tuple-element.614), kind=kOutput, calls=%fused_computation.13.clone.1 | convolution fusion | flops 805306368 | bytes 4063744 | tf_op jit(solution)/shard_map/while/body/eval_jaxpr/rc,bck->rbk/dot_general | solution.py:19
  148.4 3.0 %fusion.96 = f32[512,1,128]{2,1,0:T(1,128)S(1)} fusion(bf16[16,512,1]{0,2,1:T(2,128)(2,1)S(1)} %copy.53, bf16[512,16,128]{2,0,1:T(8,128)(2,1)} %fusion.95), kind=kOutput, calls=%fused_computation.11.clone.1 | convolution fusion | flops 2097152 | bytes 2375680 | tf_op jit(solution)/shard_map/while/body/eval_jaxpr/br,rbk->rk/dot_general | solution.py:20
  152.1 1.1 add.108
  153.2 7.6 %gather_fusion.3 = f32[2048,128]{1,0:T(8,128)} fusion(f32[1024,128]{1,0:T(8,128)S(1)} %bitcast.151, s32[2048]{0:T(1024)S(1)} %broadcast_clamp_fusion.1), kind=kCustom, calls=%fused_computation.3 | custom fusion | bytes 2105344 | tf_op jit(solution)/shard_map/gather | solution.py:110
  160.8 7.6 %gather_fusion.4 = f32[2048,128]{1,0:T(8,128)} fusion(f32[1024,128]{1,0:T(8,128)S(1)} %bitcast.152, s32[2048]{0:T(1024)S(1)} %broadcast_clamp_fusion), kind=kCustom, calls=%fused_computation.4 | custom fusion | bytes 2105344 | tf_op jit(solution)/shard_map/gather | solution.py:111
  168.4 2.9 %add_convert_fusion = bf16[128,16,128]{2,1,0:T(8,128)(2,1)} fusion(f32[128,16,128]{2,1,0:T(8,128)} %bitcast.160, f32[128,16,128]{2,1,0:T(8,128)} %bitcast.159, f32[128,16]{1,0:T(8,128)S(1)} %mul.129, f32[128,16]{1,0:T(8,128)S(1)} %mul.118), kind=kLoop, calls=%fused_computation.87 | loop fusion | flops 1048576 | bytes 2637824 | tf_op jit(solution)/shard_map/convert_element_type | solution.py:112
  171.4 4.6 %all-to-all-start.1 = ((bf16[128,16,128]{2,1,0:T(8,128)(2,1)}), bf16[128,16,128]{2,1,0:T(8,128)(2,1)S(1)}, u32[]{:S(2)}, u32[]{:S(2)}) async-start(bf16[128,16,128]{2,1,0:T(8,128)(2,1)} %add_convert_fusion), calls=%async_computation.1 | async-start | bytes 1048576 | tf_op jit(solution)/shard_map/all_to_all | solution.py:118
  176.0 1.3 broadcast.138.clone
  177.3 7.3 %while.66 = (s32[]{:T(128)}, f32[2,512,384]{2,1,0:T(8,128)}, f32[2,16,512]{2,1,0:T(8,128)S(1)}, f32[2,512,128]{2,1,0:T(8,128)S(1)}, bf16[16,384,128]{2,1,0:T(8,128)(2,1)}, /*index=5*/s32[]{:T(128)}) while((s32[]{:T(128)}, f32[2,512,384]{2,1,0:T(8,128)}, f32[2,16,512]{2,1,0:T(8,128)S(1)}, f32[2,512,128]{2,1,0:T(8,128)S(1)}, ...), condition=%wide.region_8.9_spmd, body=%wide.region_7.8_spmd.sunk | while | flops 807403520 | bytes 3244621 | solution.py:35
  177.3 3.6 %fusion.104 = f32[2,512,384]{2,1,0:T(8,128)} fusion(f32[2,512,384]{2,1,0:T(8,128)} %get-tuple-element.675, s32[]{:T(128)} %get-tuple-element.674, bf16[16,384,128]{2,1,0:T(8,128)(2,1)} %get-tuple-element.684, f32[512,128]{1,0:T(8,128)S(1)} %dynamic-slice_bitcast_fusion.14, f32[512,16]{0,1:T(8,128)S(1)} %dynamic-slice_bitcast_fusion.15), kind=kOutput, calls=%fused_computation.32.clone.1 | convolution fusion | flops 807403520 | bytes 2654720 | tf_op jit(solution)/shard_map/while/body/eval_jaxpr/rbk,bck->rc/dot_general | solution.py:33
  181.0 3.6 %fusion.104 = f32[2,512,384]{2,1,0:T(8,128)} fusion(f32[2,512,384]{2,1,0:T(8,128)} %get-tuple-element.675, s32[]{:T(128)} %get-tuple-element.674, bf16[16,384,128]{2,1,0:T(8,128)(2,1)} %get-tuple-element.684, f32[512,128]{1,0:T(8,128)S(1)} %dynamic-slice_bitcast_fusion.14, f32[512,16]{0,1:T(8,128)S(1)} %dynamic-slice_bitcast_fusion.15), kind=kOutput, calls=%fused_computation.32.clone.1 | convolution fusion | flops 807403520 | bytes 2654720 | tf_op jit(solution)/shard_map/while/body/eval_jaxpr/rbk,bck->rc/dot_general | solution.py:33
  184.6 2.0 add.114
  186.6 9.0 %while.69 = (s32[]{:T(128)}, f32[2048,384]{1,0:T(8,128)}, s32[2,512]{1,0:T(2,128)S(1)}, f32[2,512]{1,0:T(2,128)S(1)}, s32[2,512]{1,0:T(2,128)S(1)}, /*index=5*/bf16[2,512,384]{2,1,0:T(8,128)(2,1)S(1)}, s32[]{:T(128)}, s32[]{:T(128)}) while((s32[]{:T(128)}, f32[2048,384]{1,0:T(8,128)}, s32[2,512]{1,0:T(2,128)S(1)}, ...), condition=%wide.region_12.13_spmd.clone.clone, body=%wide.region_11.12_spmd.clone.clone.sunk | while | flops 812122624 | bytes 6709355 | solution.py:62
  186.7 3.5 %select_add_fusion.2 = f32[2048,384]{1,0:T(8,128)} fusion(f32[2048,384]{1,0:T(8,128)} %get-tuple-element.713, f32[512]{0:T(512)S(1)} %broadcast_subtract_fusion.7, s32[512]{0:T(512)S(1)} %bitcast.172, f32[512]{0:T(512)S(1)} %bitcast.169, s32[512]{0:T(512)S(1)} %bitcast.173, pred[]{:T(512)S(6)} %compare.7, ...), kind=kOutput, calls=%fused_computation.69.clone.1 | convolution fusion | flops 812122112 | bytes 6692869 | tf_op jit(solution)/shard_map/while/body/eval_jaxpr/nt,nw->tw/dot_general | solution.py:52
  190.2 5.4 %select_add_fusion.2 = f32[2048,384]{1,0:T(8,128)} fusion(f32[2048,384]{1,0:T(8,128)} %get-tuple-element.713, f32[512]{0:T(512)S(1)} %broadcast_subtract_fusion.7, s32[512]{0:T(512)S(1)} %bitcast.172, f32[512]{0:T(512)S(1)} %bitcast.169, s32[512]{0:T(512)S(1)} %bitcast.173, pred[]{:T(512)S(6)} %compare.7, ...), kind=kOutput, calls=%fused_computation.69.clone.1 | convolution fusion | flops 812122112 | bytes 6692869 | tf_op jit(solution)/shard_map/while/body/eval_jaxpr/nt,nw->tw/dot_general | solution.py:52
  195.6 3.0 %copy.33 = bf16[2048,384]{0,1:T(8,128)(2,1)} copy(f32[2048,384]{1,0:T(8,128)} %get-tuple-element.195) | data formatting | bytes 4718592 | tf_op jit(solution)/shard_map/while | solution.py:62
  198.7 4.1 %copy.34 = bf16[2048,3,128]{2,1,0:T(4,128)(2,1)} copy(bf16[2048,3,128]{0,2,1:T(8,128)(2,1)} %bitcast.158) | data formatting | bytes 3145728 | tf_op jit(solution)/shard_map/reshape | solution.py:116
  202.8 10.3 %all-to-all-start.3 = ((bf16[2048,3,128]{2,1,0:T(4,128)(2,1)}), bf16[2048,3,128]{2,1,0:T(4,128)(2,1)}, u32[]{:S(2)}, u32[]{:S(2)}) async-start(bf16[2048,3,128]{2,1,0:T(4,128)(2,1)} %copy.34), calls=%async_computation.3 | async-start | bytes 4194304 | tf_op jit(solution)/shard_map/all_to_all | solution.py:119
  213.2 8.0 %scatter_custom_fusion = s32[2048]{0:T(1024)S(1)} fusion(s32[2048]{0:T(1024)S(1)} %bitcast.175, s32[2048]{0:T(1024)S(1)} %iota.13, s32[]{:T(128)} %constant.84.clone.1), kind=kCustom, calls=%fused_computation.102 | custom fusion | bytes 8196 | tf_op jit(solution)/shard_map/scatter | solution.py:122
  221.3 8.1 %gather_fusion.5 = bf16[2048,128]{1,0:T(8,128)(2,1)} fusion(bf16[2048,128]{1,0:T(8,128)(2,1)S(1)} %bitcast.153, s32[2048]{0:T(1024)S(1)} %fusion.59), kind=kCustom, calls=%fused_computation.5 | custom fusion | bytes 1056768 | tf_op jit(solution)/shard_map/gather | solution.py:124
  229.3 13.2 %all-to-all-done.3 = bf16[2048,3,128]{2,1,0:T(4,128)(2,1)} async-done(((bf16[2048,3,128]{2,1,0:T(4,128)(2,1)}), bf16[2048,3,128]{2,1,0:T(4,128)(2,1)}, u32[]{:S(2)}, u32[]{:S(2)}) %all-to-all-start.3) | async-done | bytes 1572896 | tf_op jit(solution)/shard_map/all_to_all | solution.py:119
  242.5 16.1 %gather_fusion.7 = bf16[2048,3,128]{2,1,0:T(4,128)(2,1)} fusion(bf16[2048,3,128]{2,1,0:T(4,128)(2,1)} %all-to-all-done.3, s32[2048]{0:T(1024)S(1)} %fusion.59), kind=kCustom, calls=%fused_computation.7 | custom fusion | bytes 3153920 | tf_op jit(solution)/shard_map/gather | solution.py:125
  258.6 3.0 %copy.35 = bf16[2048,3,128]{2,0,1:T(8,128)(2,1)} copy(bf16[2048,3,128]{2,1,0:T(4,128)(2,1)} %gather_fusion.7) | data formatting | bytes 3145728
  (102 shorter events, 9.3 us)
Async XLA Ops:
  7.2 22.9 %copy-start = (bf16[2048,3,128]{2,0,1:T(8,128)(2,1)S(1)}, bf16[2048,3,128]{2,0,1:T(8,128)(2,1)}, u32[]{:S(2)}) copy-start(bf16[2048,3,128]{2,0,1:T(8,128)(2,1)} %param.24) | copy-start | bytes 4718596
  7.2 105.9 %all-gather.5.cloned.1.call-start = ((), (), s32[]{:S(2)}) async-start(), calls=%async_computation.5 | async-start | bytes 1462272 | tf_op jit(solution)/shard_map/all_gather | solution.py:82
  8.6 21.1 %copy-start.8 = (f32[1024]{0:T(1024)S(1)}, f32[1024]{0:T(1024)}, u32[]{:S(2)}) copy-start(f32[1024]{0:T(1024)} %param.28) | copy-start | bytes 12292
  8.6 21.1 %copy-start.3 = (f32[2048]{0:T(1024)S(1)}, f32[2048]{0:T(1024)}, u32[]{:S(2)}) copy-start(f32[2048]{0:T(1024)} %param.30) | copy-start | bytes 24580
  8.7 21.2 %copy-start.6 = (s32[2,2048]{1,0:T(2,128)S(1)}, s32[2,2048]{1,0:T(2,128)}, u32[]{:S(2)}) copy-start(s32[2,2048]{1,0:T(2,128)} %param.29) | copy-start | bytes 49156
  17.5 35.6 %all-to-all-start.2 = ((bf16[128,16,128]{2,1,0:T(8,128)(2,1)}), bf16[128,16,128]{2,1,0:T(8,128)(2,1)S(1)}, u32[]{:S(2)}, u32[]{:S(2)}) async-start(bf16[128,16,128]{2,1,0:T(8,128)(2,1)} %bitcast.45), calls=%async_computation.2 | async-start | bytes 1048576 | tf_op jit(solution)/shard_map/all_to_all | solution.py:93
  29.0 106.0 %all-gather.3.cloned.1.call-start = ((), (), s32[]{:S(2)}) async-start(), calls=%async_computation.4 | async-start | bytes 1671168 | tf_op jit(solution)/shard_map/all_gather | solution.py:81
  48.4 4.2 %copy-start.7 = (s32[2,1024]{1,0:T(2,128)S(1)}, s32[2,1024]{1,0:T(2,128)}, u32[]{:S(2)}) copy-start(s32[2,1024]{1,0:T(2,128)} %param.27) | copy-start | bytes 24580
  48.4 4.3 %copy-start.9 = (s32[1024]{0:T(1024)S(1)}, s32[1024]{0:T(1024)}, u32[]{:S(2)}) copy-start(s32[1024]{0:T(1024)} %param.33) | copy-start | bytes 12292
  48.4 4.3 %copy-start.4 = (f32[14,1024]{1,0:T(8,128)S(1)}, f32[14,1024]{1,0:T(8,128)}, u32[]{:S(2)}) copy-start(f32[14,1024]{1,0:T(8,128)} %param.32) | copy-start | bytes 172036
  48.4 4.4 %copy-start.5 = (f32[16,1024]{1,0:T(8,128)S(1)}, f32[16,1024]{1,0:T(8,128)}, u32[]{:S(2)}) copy-start(f32[16,1024]{1,0:T(8,128)} %param.31) | copy-start | bytes 196612
  53.1 41.2 %all-to-all-start = ((bf16[2048,3,128]{2,1,0:T(4,128)(2,1)}), bf16[2048,3,128]{2,1,0:T(4,128)(2,1)}, u32[]{:S(2)}, u32[]{:S(2)}) async-start(bf16[2048,3,128]{2,1,0:T(4,128)(2,1)} %copy.25), calls=%async_computation | async-start | bytes 4194304 | tf_op jit(solution)/shard_map/all_to_all | solution.py:92
  67.9 30.5 %copy-start.1 = (f32[1024,128]{1,0:T(8,128)}, f32[1024,128]{1,0:T(8,128)S(1)}, u32[]{:S(2)}) copy-start(f32[1024,128]{1,0:T(8,128)S(1)} %get-tuple-element.192) | copy-start | bytes 1572868
  110.2 4.1 %copy-start.2 = (f32[1024,128]{1,0:T(8,128)S(1)}, f32[1024,128]{1,0:T(8,128)}, u32[]{:S(2)}) copy-start(f32[1024,128]{1,0:T(8,128)} %copy-done.1) | copy-start | bytes 1572868
  171.4 31.4 %all-to-all-start.1 = ((bf16[128,16,128]{2,1,0:T(8,128)(2,1)}), bf16[128,16,128]{2,1,0:T(8,128)(2,1)S(1)}, u32[]{:S(2)}, u32[]{:S(2)}) async-start(bf16[128,16,128]{2,1,0:T(8,128)(2,1)} %add_convert_fusion), calls=%async_computation.1 | async-start | bytes 1048576 | tf_op jit(solution)/shard_map/all_to_all | solution.py:118
  202.8 39.7 %all-to-all-start.3 = ((bf16[2048,3,128]{2,1,0:T(4,128)(2,1)}), bf16[2048,3,128]{2,1,0:T(4,128)(2,1)}, u32[]{:S(2)}, u32[]{:S(2)}) async-start(bf16[2048,3,128]{2,1,0:T(4,128)(2,1)} %copy.34), calls=%async_computation.3 | async-start | bytes 4194304 | tf_op jit(solution)/shard_map/all_to_all | solution.py:119
Sparse Core Ops, SparseCore 0:
  10.1 48.2 all-gather.4
  60.5 52.2 all-gather.2
where the time goes:
time: 270 us; the launch traced here: 268 us
  local copies, waits for them, and re-layouts  111 us (41%)
  matrix products  54.9 us (20%)
  waiting for transfers between devices  41 us (15%)
  starting transfers between devices  36.8 us (14%)
  between operations  14.4 us (5%)
  other arithmetic  9.73 us (4%)
    all_to_all x1, waiting for transfers between devices, local(): lax.all_to_all(sent_fields, ('lat', 'lon'), split_axis=0, concat_axis=0,...  26.3 us
    gather x2, local copies, waits for them, and re-layouts, local(): sent_fields = increments[order_map]  22.6 us
    gather x1, local copies, waits for them, and re-layouts, local(): gradient = back_gradient[inverse_map]  16.1 us
    dot_general x4, matrix products, one_block(): jnp.einsum('rc,bck->rbk', pair[0], band_table, preferred_element_type=jnp...  16 us
    dot_general x4, matrix products, one_block(): jnp.einsum('rbk,bck->rc', lifted, band_table, preferred_element_type=jnp....  14 us
    all_to_all x1, waiting for transfers between devices, local(): lax.all_to_all(gradient_rad, ('lat', 'lon'), split_axis=0, concat_axis=0,...  13.2 us
    dot_general x6, matrix products, one_block(): jnp.einsum('nt,nw->tw', table, rows, preferred_element_type=jnp.float32)  13.2 us
    dot_general x4, matrix products, one_block(): return jnp.einsum('br,rbk->rk', pair[1], product)  11.6 us
  transfers between devices with their start and end apart: 6, of which 2 were waited for; matrix products, arithmetic and copies ran while one was open for 45% of the time, Pallas kernels for 0%

commit v1 on v0

v1 whole, which is shorter than its diff:
```python
import functools

import jax
import jax.numpy as jnp
from jax import lax
from jax.experimental import pallas as pl
from jax.experimental.pallas import tpu as pltpu
from jax.sharding import PartitionSpec as P

ALL = ("lat", "lon")
F32 = jnp.float32
BF16 = jnp.bfloat16


def columns(row, start, count):
    piece = row[:, start : start + count]
    return jnp.transpose(jnp.broadcast_to(piece, (128, count)))


def wide(column, width):
    return jnp.concatenate([column] * (width // 128), axis=1)


def pick_kernel(planes, perm_ref, *refs):
    sources, out_ref = refs[:-1], refs[-1]
    rows = out_ref.shape[0]
    total = perm_ref.shape[1]
    start = pl.multiple_of(pl.program_id(0) * rows, rows)
    index = jnp.transpose(jnp.broadcast_to(perm_ref[:, pl.ds(start, rows)], (128, rows)))
    lanes = lax.broadcasted_iota(jnp.int32, (rows, total), 1)
    hot = (wide(index, total) == lanes).astype(F32).astype(BF16)
    pieces = []
    for ref in sources:
        if len(ref.shape) == 3:
            pieces.extend(ref[v] for v in range(ref.shape[0]))
        else:
            pieces.append(ref[...])
    data = pieces[0] if len(pieces) == 1 else jnp.concatenate(pieces, axis=1)
    out_ref[...] = jnp.dot(hot, data, preferred_element_type=F32).astype(BF16)


def full(shape):
    return pl.BlockSpec(shape, lambda *_: (0,) * len(shape))


def cost(flops, nbytes):
    return pl.CostEstimate(flops=flops, bytes_accessed=nbytes, transcendentals=0)


def pick(perm, *sources):
    total = perm.shape[1]
    width = sum(s.shape[0] * s.shape[2] if s.ndim == 3 else s.shape[1] for s in sources)
    rows = 512
    return pl.pallas_call(
        functools.partial(pick_kernel, None),
        grid=(total // rows,),
        in_specs=[full(perm.shape)] + [full(s.shape) for s in sources],
        out_specs=pl.BlockSpec((rows, width), lambda i: (i, 0)),
        out_shape=jax.ShapeDtypeStruct((total, width), BF16),
        cost_estimate=cost(2 * total * total * width, 4 * total * width),
        name="pick",
    )(perm, *sources)


def restore_kernel(perm_ref, data_ref, out_ref):
    rows = out_ref.shape[-2]
    total = perm_ref.shape[1]
    start = pl.program_id(0) * rows
    targets = lax.broadcasted_iota(jnp.int32, (rows, total), 0) + start
    hot = (jnp.broadcast_to(perm_ref[...], (rows, total)) == targets).astype(F32).astype(BF16)
    got = jnp.dot(hot, data_ref[...], preferred_element_type=F32).astype(BF16)
    if len(out_ref.shape) == 3:
        for v in range(out_ref.shape[0]):
            out_ref[v] = got[:, v * 128 : (v + 1) * 128]
    else:
        out_ref[...] = got


def restore(perm, data):
    total, width = data.shape
    rows = 512
    if width > 128:
        planes = width // 128
        out_spec = pl.BlockSpec((planes, rows, 128), lambda i: (0, i, 0))
        out_shape = jax.ShapeDtypeStruct((planes, total, 128), BF16)
    else:
        out_spec = pl.BlockSpec((rows, width), lambda i: (i, 0))
        out_shape = jax.ShapeDtypeStruct((total, width), BF16)
    return pl.pallas_call(
        restore_kernel,
        grid=(total // rows,),
        in_specs=[full(perm.shape), full(data.shape)],
        out_specs=out_spec,
        out_shape=out_shape,
        cost_estimate=cost(2 * total * total * width, 4 * total * width),
        name="restore",
    )(perm, data)


def two_hot_columns(first, second, share, width):
    rows = first.shape[0]
    lanes = lax.broadcasted_iota(jnp.int32, (rows, width), 1)
    one = jnp.where(wide(first, width) == lanes, wide(share, width), 0.0)
    two = jnp.where(wide(second, width) == lanes, wide(1.0 - share, width), 0.0)
    return (one + two).astype(BF16)


def two_hot_rows(first, second, share, rows, start):
    width = first.shape[1]
    targets = lax.broadcasted_iota(jnp.int32, (rows, width), 0) + start
    one = jnp.where(jnp.broadcast_to(first, (rows, width)) == targets, share, 0.0)
    two = jnp.where(jnp.broadcast_to(second, (rows, width)) == targets, 1.0 - share, 0.0)
    return (one + two).astype(BF16)


def scale_columns(scale_ref, start, rows):
    return jnp.transpose(scale_ref[:, pl.ds(start, rows)])


def adjoint_kernel(
    cot_ref, bidx_ref, bw_ref, cidx_ref, cw_ref, scale_ref, ta_ref, tb_ref, out_ref, adj_ref, rows_ref
):
    row_count = adj_ref.shape[0]
    col_count = out_ref.shape[0]
    block = 256
    bands = ta_ref.shape[0]

    def spread(i, carry):
        start = pl.multiple_of(i * block, block)
        table = two_hot_rows(bidx_ref[0:1, :], bidx_ref[1:2, :], bw_ref[...], block, start)
        adj = jnp.dot(table, cot_ref[...], preferred_element_type=F32)
        scales = scale_columns(scale_ref, start, block)
        lifted = [
            (jnp.broadcast_to(scales[:, b : b + 1], (block, 128)) * adj).astype(BF16)
            for b in range(2 * bands)
        ]
        weights = [ta_ref[b] for b in range(bands)] + [tb_ref[b] for b in range(bands)]
        rows_ref[pl.ds(start, block), :] = lax.dot_general(
            jnp.concatenate(lifted, axis=1),
            jnp.concatenate(weights, axis=1),
            (((1,), (1,)), ((), ())),
            preferred_element_type=F32,
        ).astype(BF16)
        return carry

    lax.fori_loop(0, row_count // block, spread, 0)

    def scatter(i, carry):
        start = pl.multiple_of(i * block, block)
        table = two_hot_rows(cidx_ref[0:1, :], cidx_ref[1:2, :], cw_ref[...], block, start)
        out_ref[pl.ds(start, block), :] = jnp.dot(
            table, rows_ref[...], preferred_element_type=F32
        ).astype(BF16)
        return carry

    lax.fori_loop(0, col_count // block, scatter, 0)


def adjoint(cot, bidx, bw, cidx, cw, scale, ta, tb):
    col_count = cot.shape[0]
    row_count = cw.shape[1]
    width = ta.shape[1]
    return pl.pallas_call(
        adjoint_kernel,
        out_shape=jax.ShapeDtypeStruct((col_count, width), BF16),
        scratch_shapes=[
            pltpu.VMEM((row_count, 128), F32),
            pltpu.VMEM((row_count, width), BF16),
        ],
        cost_estimate=cost(2 * row_count * 128 * 30 * width * 2, 8 * 1024 * 1024),
        name="adjoint",
    )(cot, bidx, bw, cidx, cw, scale, ta, tb)


def forward_kernel(
    fields_ref, bidx_ref, bw_ref, cidx_ref, cw_ref, scale_ref, ta_ref, tb_ref, out_ref, heat_ref
):
    row_count = heat_ref.shape[0]
    col_count = out_ref.shape[0]
    block = 256
    bands = ta_ref.shape[0]

    def band(i, carry):
        start = pl.multiple_of(i * block, block)
        get = lambda ref, k: jnp.transpose(
            jnp.broadcast_to(ref[k : k + 1, pl.ds(start, block)], (128, block))
        )
        table = two_hot_columns(get(cidx_ref, 0), get(cidx_ref, 1), get(cw_ref, 0), col_count)
        coarse = jnp.dot(table, fields_ref[...], preferred_element_type=F32).astype(BF16)
        scales = scale_columns(scale_ref, start, block)
        weights = [ta_ref[b] for b in range(bands)] + [tb_ref[b] for b in range(bands)]
        heat = jnp.zeros((block, 128), F32)
        for pair in range(bands):
            both = jnp.concatenate(weights[2 * pair : 2 * pair + 2], axis=1)
            product = jnp.dot(coarse, both, preferred_element_type=F32)
            for half in range(2):
                b = 2 * pair + half
                heat = heat + jnp.broadcast_to(scales[:, b : b + 1], (block, 128)) * product[
                    :, half * 128 : (half + 1) * 128
                ]
        heat_ref[pl.ds(start, block), :] = heat.astype(BF16)
        return carry

    lax.fori_loop(0, row_count // block, band, 0)

    def back(i, carry):
        start = pl.multiple_of(i * block, block)
        get = lambda ref, k: jnp.transpose(
            jnp.broadcast_to(ref[k : k + 1, pl.ds(start, block)], (128, block))
        )
        table = two_hot_columns(get(bidx_ref, 0), get(bidx_ref, 1), get(bw_ref, 0), row_count)
        out_ref[pl.ds(start, block), :] = jnp.dot(
            table, heat_ref[...], preferred_element_type=F32
        ).astype(BF16)
        return carry

    lax.fori_loop(0, col_count // block, back, 0)


def forward(fields, bidx, bw, cidx, cw, scale, ta, tb):
    col_count = fields.shape[0]
    row_count = cw.shape[1]
    return pl.pallas_call(
        forward_kernel,
        out_shape=jax.ShapeDtypeStruct((col_count, 128), BF16),
        scratch_shapes=[pltpu.VMEM((row_count, 128), BF16)],
        cost_estimate=cost(2 * row_count * 128 * 30 * fields.shape[1] * 2, 8 * 1024 * 1024),
        name="forward",
    )(fields, bidx, bw, cidx, cw, scale, ta, tb)


def exchange(values, axes):
    return lax.all_to_all(values, axes, split_axis=0, concat_axis=0, tiled=True)


def local(
    increments,
    cotangent,
    owner_perm,
    coarse_index,
    coarse_weight,
    back_index,
    back_weight,
    lw_scale,
    sw_scale,
    sunlit,
    lw_table,
    sw_table,
):
    lat, lon = lax.axis_size("lat"), lax.axis_size("lon")
    core = lax.rem(lax.axis_index("lat"), 2)
    table = jnp.concatenate([lw_table, sw_table], axis=0)
    bands, variables, depth, levels = table.shape
    half = bands // 2
    mine = lax.dynamic_slice_in_dim(table, core * half, half, axis=0)
    mine = jnp.broadcast_to(mine[None], (lon,) + mine.shape)
    got = exchange(mine, ("lon",))
    got = got.transpose(1, 2, 0, 3, 4).reshape(half, variables * lon * depth, levels)
    partner = [(a, a + 1 - 2 * (a % 2)) for a in range(lat)]
    other = lax.ppermute(got, "lat", partner)
    scale = jnp.concatenate([lw_scale, sw_scale * sunlit.astype(F32)[None, :]], axis=0)
    scale = jnp.where(core == 0, scale, jnp.roll(scale, half, axis=0))
    scale = jnp.pad(scale, ((0, 2), (0, 0)))

    cw = coarse_weight[None]
    bw = back_weight[None]
    planes = increments.transpose(1, 0, 2)
    cot_rad = exchange(pick(owner_perm, cotangent), ALL)
    fields = exchange(pick(owner_perm, planes), ALL)
    gradient_rad = adjoint(cot_rad, back_index, bw, coarse_index, cw, scale, got, other)
    back_gradient = exchange(gradient_rad, ALL)
    tendency_rad = forward(fields, back_index, bw, coarse_index, cw, scale, got, other)
    back_tendency = exchange(tendency_rad, ALL)
    gradient = restore(owner_perm, back_gradient).transpose(1, 0, 2)
    tendency = restore(owner_perm, back_tendency)
    return (tendency, gradient)


def solution(mesh):
    in_specs = (
        P(ALL, None, None),
        P(ALL, None),
        P(ALL, None),
        P(None, ALL),
        P(ALL),
        P(None, ALL),
        P(ALL),
        P(None, ALL),
        P(None, ALL),
        P(ALL),
        P(None, None, "lon", None),
        P(None, None, "lon", None),
    )
    out_specs = (P(ALL, None), P(ALL, None, None))
    return jax.shard_map(local, mesh=mesh, in_specs=in_specs, out_specs=out_specs, check_vma=False)
```

time: 270 us -> 152 us (0.56)
  local copies, waits for them, and re-layouts: 111 us -> 5.54 us
  matrix products: 54.9 us -> 0 us
  Pallas kernels: 0 us -> 52.8 us
  between operations: 14.4 us -> 0.76 us
  waiting for transfers between devices: 41 us -> 49.9 us
  other arithmetic: 9.73 us -> 1.02 us
  starting transfers between devices: 36.8 us -> 41.2 us
    gather x9 -> x0, local copies, waits for them, and re-layouts: 80.8 us -> none  [the longest x2 22.6 us: local(): sent_fields = increments[order_map]]
    dot_general x18 -> x0, matrix products: 54.9 us -> none  [the longest x4 16 us: one_block(): jnp.einsum('rc,bck->rbk', pair[0], band_table, preferred_element_type=jnp...]
    pallas_call x0 -> x6, Pallas kernels: none -> 52.8 us  [the longest x1 15.2 us: forward(): pl.pallas_call(forward_kernel, out_shape=jax.ShapeDtypeStruct((col_count,...]
    all_to_all x4 -> x5, waiting for transfers between devices: 39.6 us -> 49.9 us  [exchange(): return lax.all_to_all(values, axes, split_axis=0, concat_axis=0, tiled=True)]
    scatter x1 -> x0, local copies, waits for them, and re-layouts: 8.05 us -> none  [local(): jnp.zeros((col_count,), jnp.int32).at[order_map]]
    reshape x5 -> x0, local copies, waits for them, and re-layouts: 6.13 us -> none  [the longest x1 4.14 us: local(): gradient_rad = gradient_rad.reshape(increments.shape)]
    convert_element_type x3 -> x1, other arithmetic: 5.76 us -> 0.01 us  [local(): sunlit.astype(F32)[None, :]]
    all_to_all x1 -> x0, local copies, waits for them, and re-layouts: 4.09 us -> none  [local(): lax.all_to_all(sent_fields, ('lat', 'lon'), split_axis=0, concat_axis=0,...]
  transfers between devices with their start and end apart: 6 -> 6, of which waited for: 2 -> 4; matrix products, arithmetic and copies ran while one was open for 45% -> 1% of each run, Pallas kernels for 0% -> 30%
where the time goes in v1:
time: 152 us; the launch traced here: 151 us
  Pallas kernels  52.8 us (35%)
  waiting for transfers between devices  49.9 us (33%)
  starting transfers between devices  41.2 us (27%)
  local copies, waits for them, and re-layouts  5.54 us (4%)
    all_to_all x5, waiting for transfers between devices, exchange(): return lax.all_to_all(values, axes, split_axis=0, concat_axis=0, tiled=True)  49.9 us
    all_to_all x5, starting transfers between devices, exchange(): return lax.all_to_all(values, axes, split_axis=0, concat_axis=0, tiled=True)  40.2 us
    pallas_call x1, Pallas kernels, forward(): pl.pallas_call(forward_kernel, out_shape=jax.ShapeDtypeStruct((col_count,...  15.2 us
    pallas_call x1, Pallas kernels, adjoint(): pl.pallas_call(adjoint_kernel, out_shape=jax.ShapeDtypeStruct((col_count,...  13.6 us
    pallas_call x2, Pallas kernels, pick(): pl.pallas_call(functools.partial(pick_kernel, None), grid=(total // rows,...  12.2 us
    pallas_call x2, Pallas kernels, restore(): pl.pallas_call(restore_kernel, grid=(total // rows,), in_specs=[full(perm...  11.8 us
  transfers between devices with their start and end apart: 6, of which 4 were waited for; matrix products, arithmetic and copies ran while one was open for 1% of the time, Pallas kernels for 30%

profile of v1, /device:TPU:1, one launch (start us, length us, event | category | flops | bytes accessed | tf_op | source)
XLA Modules:
  0.0 151.3 jit_solution(1196210755798240299)
XLA Ops:
  0.6 1.0 fusion.1
  1.6 1.3 broadcast_in_dim.15
  2.9 7.6 %all-to-all-start.1 = ((bf16[16,15,3,8,128]{4,3,2,1,0:T(8,128)(2,1)}), bf16[16,15,3,8,128]{4,3,2,1,0:T(8,128)(2,1)S(1)}, u32[]{:S(2)}, u32[]{:S(2)}) async-start(bf16[16,15,3,8,128]{4,3,2,1,0:T(8,128)(2,1)} %broadcast_in_dim.15), calls=%async_computation.1 | async-start | bytes 2949120 | tf_op jit(solution)/shard_map/all_to_all | solution.py:233
  10.5 7.4 %pick.2 = bf16[2048,384]{1,0:T(8,128)(2,1)} custom-call(s32[1,2048]{1,0:T(1,128)} %perm_ref.7, bf16[3,2048,128]{2,1,0:T(8,128)(2,1)} %bitcast.23), custom_call_target="tpu_custom_call" | custom-call | flops 3221225472 | bytes 3145728 | tf_op jit(solution)/shard_map/pick/pallas_call | solution.py:54
  17.9 14.3 %all-to-all-done.1 = bf16[16,15,3,8,128]{4,3,2,1,0:T(8,128)(2,1)S(1)} async-done(((bf16[16,15,3,8,128]{4,3,2,1,0:T(8,128)(2,1)}), bf16[16,15,3,8,128]{4,3,2,1,0:T(8,128)(2,1)S(1)}, u32[]{:S(2)}, u32[]{:S(2)}) %all-to-all-start.1) | async-done | bytes 1474592 | tf_op jit(solution)/shard_map/all_to_all | solution.py:233
  32.2 8.3 %all-to-all-start = ((bf16[128,16,384]{2,1,0:T(8,128)(2,1)}), bf16[128,16,384]{2,1,0:T(8,128)(2,1)S(1)}, u32[]{:S(2)}, u32[]{:S(2)}) async-start(bf16[128,16,384]{2,1,0:T(8,128)(2,1)} %bitcast.16), calls=%async_computation | async-start | bytes 3145728 | tf_op jit(solution)/shard_map/all_to_all | solution.py:233
  40.5 0.0 copy-start.6
  40.5 0.0 copy-start.5
  40.6 0.0 copy-start.2
  40.6 1.6 %copy.14 = bf16[15,3,16,8,128]{4,3,2,1,0:T(8,128)(2,1)} copy(bf16[15,3,16,8,128]{4,3,1,0,2:T(8,128)(2,1)S(1)} %bitcast.14) | data formatting | bytes 2949120 | tf_op jit(solution)/shard_map/transpose | solution.py:258
  42.1 1.1 collective-permute-start
  43.2 0.0 copy-done.6
  43.2 0.0 copy-done.5
  43.2 0.0 copy-done.2
  43.3 0.7 pad.4.scale_ref
  43.9 4.8 %pick.3 = bf16[2048,128]{1,0:T(8,128)(2,1)} custom-call(s32[1,2048]{1,0:T(1,128)} %perm_ref.7, bf16[2048,128]{1,0:T(8,128)(2,1)} %refs_0_.1), custom_call_target="tpu_custom_call" | custom-call | flops 1073741824 | bytes 1048576 | tf_op jit(solution)/shard_map/pick/pallas_call | solution.py:54
  48.7 15.9 %all-to-all-done = bf16[128,16,384]{2,1,0:T(8,128)(2,1)S(1)} async-done(((bf16[128,16,384]{2,1,0:T(8,128)(2,1)}), bf16[128,16,384]{2,1,0:T(8,128)(2,1)S(1)}, u32[]{:S(2)}, u32[]{:S(2)}) %all-to-all-start) | async-done | bytes 1572896 | tf_op jit(solution)/shard_map/all_to_all | solution.py:233
  64.6 0.0 copy-start
  64.6 4.9 %all-to-all-start.3 = ((bf16[128,16,128]{2,1,0:T(8,128)(2,1)}), bf16[128,16,128]{2,1,0:T(8,128)(2,1)S(1)}, u32[]{:S(2)}, u32[]{:S(2)}) async-start(bf16[128,16,128]{2,1,0:T(8,128)(2,1)} %bitcast.22), calls=%async_computation.3 | async-start | bytes 1048576 | tf_op jit(solution)/shard_map/all_to_all | solution.py:233
  69.5 0.0 collective-permute-done.tb_ref
  69.5 0.0 copy-done
  69.5 15.2 %forward.1 = bf16[2048,128]{1,0:T(8,128)(2,1)} custom-call(bf16[2048,384]{1,0:T(8,128)(2,1)} %bitcast.15, s32[2,2048]{1,0:T(2,128)} %bidx_ref.3, f32[1,2048]{1,0:T(1,128)} %bitcast.24, s32[2,1024]{1,0:T(2,128)} %cidx_ref.3, f32[1,1024]{1,0:T(1,128)} %bitcast.26, f32[32,1024]{1,0:T(8,128)} %pad.4.scale_ref, bf16[15,384,128]{2,1,0:T(8,128)(2,1)} %bitcast.6.ta_ref, ...), custom_call_target="tpu_custom_call" | custom-call | flops 6039797760 | bytes 8388608 | tf_op jit(solution)/shard_map/forward/pallas_call | solution.py:223
  84.7 0.0 all-to-all-done.3
  84.7 0.0 copy-start.3
  84.7 9.9 %all-to-all-start.2 = ((bf16[128,16,128]{2,1,0:T(8,128)(2,1)}), bf16[128,16,128]{2,1,0:T(8,128)(2,1)S(1)}, u32[]{:S(2)}, u32[]{:S(2)}) async-start(bf16[128,16,128]{2,1,0:T(8,128)(2,1)} %bitcast.21), calls=%async_computation.2 | async-start | bytes 1048576 | tf_op jit(solution)/shard_map/all_to_all | solution.py:233
  94.6 0.0 copy-done.3
  94.6 13.6 %adjoint.1 = bf16[2048,384]{1,0:T(8,128)(2,1)} custom-call(bf16[2048,128]{1,0:T(8,128)(2,1)} %bitcast.19, s32[2,2048]{1,0:T(2,128)} %bidx_ref.3, f32[1,2048]{1,0:T(1,128)} %bitcast.25, s32[2,1024]{1,0:T(2,128)} %cidx_ref.3, f32[1,1024]{1,0:T(1,128)} %bitcast.27, f32[32,1024]{1,0:T(8,128)} %pad.4.scale_ref, bf16[15,384,128]{2,1,0:T(8,128)(2,1)} %bitcast.6.ta_ref, ...), custom_call_target="tpu_custom_call" | custom-call | flops 6039797760 | bytes 8388608 | tf_op jit(solution)/shard_map/adjoint/pallas_call | solution.py:163
  108.3 0.3 all-to-all-done.2
  108.5 0.0 copy-start.4
  108.5 0.8 copy-done.4
  109.3 9.5 %all-to-all-start.4 = ((bf16[128,16,384]{2,1,0:T(8,128)(2,1)}), bf16[128,16,384]{2,1,0:T(8,128)(2,1)S(1)}, u32[]{:S(2)}, u32[]{:S(2)}) async-start(bf16[128,16,384]{2,1,0:T(8,128)(2,1)} %bitcast.17), calls=%async_computation.4 | async-start | bytes 3145728 | tf_op jit(solution)/shard_map/all_to_all | solution.py:233
  118.9 4.6 %restore.2 = bf16[2048,128]{1,0:T(8,128)(2,1)} custom-call(s32[1,2048]{1,0:T(1,128)} %perm_ref.7, bf16[2048,128]{1,0:T(8,128)(2,1)} %bitcast.20), custom_call_target="tpu_custom_call" | custom-call | flops 1073741824 | bytes 1048576 | tf_op jit(solution)/shard_map/restore/pallas_call | solution.py:89
  123.5 19.4 %all-to-all-done.4 = bf16[128,16,384]{2,1,0:T(8,128)(2,1)S(1)} async-done(((bf16[128,16,384]{2,1,0:T(8,128)(2,1)}), bf16[128,16,384]{2,1,0:T(8,128)(2,1)S(1)}, u32[]{:S(2)}, u32[]{:S(2)}) %all-to-all-start.4) | async-done | bytes 1572896 | tf_op jit(solution)/shard_map/all_to_all | solution.py:233
  142.9 0.0 copy-start.1
  142.9 1.2 copy-done.1
  144.1 7.2 %restore.3 = bf16[3,2048,128]{2,1,0:T(8,128)(2,1)} custom-call(s32[1,2048]{1,0:T(1,128)} %perm_ref.7, bf16[2048,384]{1,0:T(8,128)(2,1)} %bitcast.18), custom_call_target="tpu_custom_call" | custom-call | flops 3221225472 | bytes 3145728 | tf_op jit(solution)/shard_map/restore/pallas_call | solution.py:89
  (4 shorter events, 0.1 us)
Async XLA Ops:
  2.9 29.3 %all-to-all-start.1 = ((bf16[16,15,3,8,128]{4,3,2,1,0:T(8,128)(2,1)}), bf16[16,15,3,8,128]{4,3,2,1,0:T(8,128)(2,1)S(1)}, u32[]{:S(2)}, u32[]{:S(2)}) async-start(bf16[16,15,3,8,128]{4,3,2,1,0:T(8,128)(2,1)} %broadcast_in_dim.15), calls=%async_computation.1 | async-start | bytes 2949120 | tf_op jit(solution)/shard_map/all_to_all | solution.py:233
  32.2 32.4 %all-to-all-start = ((bf16[128,16,384]{2,1,0:T(8,128)(2,1)}), bf16[128,16,384]{2,1,0:T(8,128)(2,1)S(1)}, u32[]{:S(2)}, u32[]{:S(2)}) async-start(bf16[128,16,384]{2,1,0:T(8,128)(2,1)} %bitcast.16), calls=%async_computation | async-start | bytes 3145728 | tf_op jit(solution)/shard_map/all_to_all | solution.py:233
  40.5 2.7 %copy-start.6 = (s32[1024]{0:T(1024)S(1)}, s32[1024]{0:T(1024)}, u32[]{:S(2)}) copy-start(s32[1024]{0:T(1024)} %param.21) | copy-start | bytes 12292
  40.5 2.7 %copy-start.5 = (f32[14,1024]{1,0:T(8,128)S(1)}, f32[14,1024]{1,0:T(8,128)}, u32[]{:S(2)}) copy-start(f32[14,1024]{1,0:T(8,128)} %param.20) | copy-start | bytes 172036
  40.6 2.7 %copy-start.2 = (f32[16,1024]{1,0:T(8,128)S(1)}, f32[16,1024]{1,0:T(8,128)}, u32[]{:S(2)}) copy-start(f32[16,1024]{1,0:T(8,128)} %param.19) | copy-start | bytes 196612
  42.1 27.4 %collective-permute-start = (bf16[15,384,128]{2,1,0:T(8,128)(2,1)}, bf16[15,384,128]{2,1,0:T(8,128)(2,1)}, u32[]{:S(2)}, u32[]{:S(2)}) collective-permute-start(bf16[15,384,128]{2,1,0:T(8,128)(2,1)} %bitcast.6.ta_ref), channel_id=1, source_target_pairs={{0,16},{16,0},{32,48},{48,32},{64,80},{80,64},{96,112},{112,96},{1... | collective-permute-start | bytes 4423688 | tf_op jit(solution)/shard_map/ppermute | solution.py:260
  64.6 4.9 %copy-start = (bf16[128,16,384]{2,1,0:T(8,128)(2,1)}, bf16[128,16,384]{2,1,0:T(8,128)(2,1)S(1)}, u32[]{:S(2)}) copy-start(bf16[128,16,384]{2,1,0:T(8,128)(2,1)S(1)} %all-to-all-done) | copy-start | bytes 4718596
  64.6 20.1 %all-to-all-start.3 = ((bf16[128,16,128]{2,1,0:T(8,128)(2,1)}), bf16[128,16,128]{2,1,0:T(8,128)(2,1)S(1)}, u32[]{:S(2)}, u32[]{:S(2)}) async-start(bf16[128,16,128]{2,1,0:T(8,128)(2,1)} %bitcast.22), calls=%async_computation.3 | async-start | bytes 1048576 | tf_op jit(solution)/shard_map/all_to_all | solution.py:233
  84.7 9.9 %copy-start.3 = (bf16[128,16,128]{2,1,0:T(8,128)(2,1)}, bf16[128,16,128]{2,1,0:T(8,128)(2,1)S(1)}, u32[]{:S(2)}) copy-start(bf16[128,16,128]{2,1,0:T(8,128)(2,1)S(1)} %all-to-all-done.3) | copy-start | bytes 1572868
  84.7 23.8 %all-to-all-start.2 = ((bf16[128,16,128]{2,1,0:T(8,128)(2,1)}), bf16[128,16,128]{2,1,0:T(8,128)(2,1)S(1)}, u32[]{:S(2)}, u32[]{:S(2)}) async-start(bf16[128,16,128]{2,1,0:T(8,128)(2,1)} %bitcast.21), calls=%async_computation.2 | async-start | bytes 1048576 | tf_op jit(solution)/shard_map/all_to_all | solution.py:233
  108.5 0.8 copy-start.4
  109.3 33.6 %all-to-all-start.4 = ((bf16[128,16,384]{2,1,0:T(8,128)(2,1)}), bf16[128,16,384]{2,1,0:T(8,128)(2,1)S(1)}, u32[]{:S(2)}, u32[]{:S(2)}) async-start(bf16[128,16,384]{2,1,0:T(8,128)(2,1)} %bitcast.17), calls=%async_computation.4 | async-start | bytes 3145728 | tf_op jit(solution)/shard_map/all_to_all | solution.py:233
  142.9 1.2 copy-start.1
